TPU v7x, 32 devices: a whole 2x2x4 slice. The times are simulated.
32 devices in a mesh: rows: 8 (over z, x), rep: 4 (over y, core).
Axes of the slice: x: 2, y: 2, z: 4, core: 2. Of those that a mesh axis runs over, the one named last changes fastest.
Arguments:
- requests: int32 [32, 8, 128], P(('rows', 'rep')), may hold values from 0 to 1023
- request_counts: int32 [32, 8], P(('rows', 'rep')), may hold values from 0 to 128, as said below
- table: bfloat16 [8192, 512], P('rows')
- gain: float32 [512], replicated, may hold values from 0.5 to 1.5
Outputs:
- normalized: bfloat16 [32, 8, 128, 512], P(('rows', 'rep'))
- row_counts: int32 [8192], P('rows')
- moments: float32 [2, 2], replicated
Inputs may be any that keep to these rules, and one draw needn't show every extreme that they name: Each device uses request_counts[d, o] of its 128 slots toward owner o; in every draw one owner's slots are full from every device.
All inputs are finite; a program needn't handle non-finite values.
Results may differ from a plain program's by a relative error of at most 0.0004.
Values may be sent and summed in bfloat16 or wider, within the bound.
No kernel may reach another device: no remote copies, remote signals or barrier semaphores. Data moves between devices by JAX's collectives and lax.ppermute only.
A program may use at most 64 MiB of HBM per device.

v0:
```python
import functools

import jax
import jax.numpy as jnp
from jax import lax
from jax.experimental import pallas as pl
from jax.experimental.pallas import tpu as pltpu
from jax.sharding import PartitionSpec as P


WIDTH = 256
LAYERS = 2
LANES = 128
SUBLANES = 8
GRANT = 16 << 20
MOST_PERMUTES = 16

epsilon = 1e-06


VMEM = pl.BlockSpec(memory_space=pltpu.VMEM)
SMEM = pl.BlockSpec(memory_space=pltpu.SMEM)
PLACED = pl.BlockSpec(memory_space=pl.ANY)


def total(a):
    return jnp.sum(jnp.sum(a, axis=1, keepdims=True), axis=0, keepdims=True)


def one_hot(match):
    return jnp.where(match, 1.0, 0.0).astype(jnp.bfloat16)


def kernel_call(body, out_shape, in_specs, out_specs, scratch=()):
    return pl.pallas_call(
        body,
        out_shape=out_shape,
        in_specs=in_specs,
        out_specs=out_specs,
        scratch_shapes=list(scratch),
        compiler_params=pltpu.CompilerParams(vmem_limit_bytes=GRANT),
    )


def row_moments_kernel(table_ref, moments_ref):
    blocks = table_ref.shape[0] // LANES
    lane = lax.broadcasted_iota(jnp.int32, (LANES, LANES), 1)
    columns = jnp.zeros((LANES, LANES), jnp.float32)
    for block in range(blocks):
        for layer in range(LAYERS):
            x = table_ref[
                block * LANES : (block + 1) * LANES, layer * WIDTH : (layer + 1) * WIDTH
            ].astype(jnp.float32)
            mean = jnp.sum(x, axis=1, keepdims=True) * (1.0 / WIDTH)
            square = jnp.sum(jnp.square(x - mean), axis=1, keepdims=True)
            columns = jnp.where(lane == layer * blocks + block, mean, columns)
            columns = jnp.where(lane == (LAYERS + layer) * blocks + block, square, columns)
    moments_ref[...] = jnp.transpose(columns)[: 2 * LAYERS * blocks]


def tally(wanted, moments_ref, high_ref, low_ref, counts_ref):
    blocks = counts_ref.shape[0]
    lane = lax.broadcasted_iota(jnp.int32, (LANES, LANES), 1)
    block_row = lax.broadcasted_iota(jnp.int32, (blocks, LANES), 0)
    upright = jnp.transpose(wanted)
    for row in range(wanted.shape[0]):
        span = slice(row * LANES, (row + 1) * LANES)
        high_ref[:, span] = one_hot(block_row == wanted[row : row + 1] // LANES)
        low_ref[span, :] = one_hot(lane == upright[:, row : row + 1] % LANES)
    weights = jnp.dot(high_ref[...], low_ref[...], preferred_element_type=jnp.float32)
    counts_ref[...] = weights.astype(jnp.int32)

    tile_row = lax.broadcasted_iota(jnp.int32, (SUBLANES, LANES), 0)
    tile_lane = lax.broadcasted_iota(jnp.int32, (SUBLANES, LANES), 1)
    count = total(weights)
    figures = jnp.where(tile_lane == 0, count, 0.0)
    for layer in range(LAYERS):
        row_mean = moments_ref[layer * blocks : (layer + 1) * blocks]
        row_square = moments_ref[(LAYERS + layer) * blocks : (LAYERS + layer + 1) * blocks]
        mean = total(weights * row_mean) / jnp.maximum(count, 1.0)
        square = total(weights * (row_square + WIDTH * jnp.square(row_mean - mean)))
        figures = jnp.where(tile_lane == 1 + layer, mean, figures)
        figures = jnp.where(tile_lane == 1 + LAYERS + layer, square, figures)
    first = figures.astype(jnp.bfloat16).astype(jnp.float32)
    second = (figures - first).astype(jnp.bfloat16).astype(jnp.float32)
    third = figures - first - second
    return jnp.where(tile_row == 0, first, jnp.where(tile_row == 1, second, third)).astype(jnp.bfloat16)


def pick(table_ref, column):
    lane = lax.broadcasted_iota(jnp.int32, (LANES, table_ref.shape[0]), 1)
    return jnp.dot(one_hot(lane == column), table_ref[...], preferred_element_type=jnp.float32).astype(jnp.bfloat16)


def put(message_ref, rows, terms=None):
    count, columns = rows.shape
    pieces = columns // LANES
    for piece in range(pieces):
        message_ref[piece * count : (piece + 1) * count, :] = rows[:, piece * LANES : (piece + 1) * LANES]
    if terms is not None:
        message_ref[pieces * count :, :] = terms


def asked_of_me(owners, wanted_ref, shifts):
    me, group = lax.axis_index("rows"), lax.axis_index("rep")
    rows = [wanted_ref[pl.ds(group * owners + lax.rem(me + shift, owners), 1), :] for shift in shifts]
    filler = [rows[0]] * (-len(rows) % SUBLANES)
    return jnp.transpose(jnp.concatenate(rows + filler, axis=0))


def first_kernel(owners, shifts, wanted_ref, table_ref, passed_ref, *message_refs):
    passed_ref[...] = wanted_ref[...]
    columns = asked_of_me(owners, wanted_ref, shifts)
    for place, message_ref in enumerate(message_refs):
        put(message_ref, pick(table_ref, columns[:, place : place + 1]))


def tally_kernel(wanted_ref, moments_ref, counts_ref, terms_ref, high_ref, low_ref):
    terms_ref[...] = tally(wanted_ref[...], moments_ref, high_ref, low_ref, counts_ref)


def serve_kernel(owners, shifts, wanted_ref, terms_ref, table_ref, *message_refs):
    columns = asked_of_me(owners, wanted_ref, shifts)
    for place, message_ref in enumerate(message_refs):
        put(message_ref, pick(table_ref, columns[:, place : place + 1]), terms_ref[...])


def serve_all_kernel(slot_count, mine_ref, wanted_ref, moments_ref, table_ref, payload_ref, counts_ref, high_ref, low_ref):
    pieces = table_ref.shape[1] // LANES
    terms = tally(wanted_ref[...], moments_ref, high_ref, low_ref, counts_ref)
    mine = jnp.transpose(mine_ref[...])
    for row in range(mine.shape[1]):
        rows = pick(table_ref, mine[:, row : row + 1]).astype(jnp.float32)
        for start in range(0, LANES, slot_count):
            peer = (row * LANES + start) // slot_count
            for piece in range(pieces):
                payload_ref[peer, piece * slot_count : (piece + 1) * slot_count, :] = rows[
                    start : start + slot_count, piece * LANES : (piece + 1) * LANES
                ].astype(jnp.bfloat16)
    for peer in range(payload_ref.shape[0]):
        payload_ref[peer, pieces * slot_count :, :] = terms


def merge(figures, moments_ref):
    counts = figures[:, 0:1]
    entries = jnp.sum(counts, axis=0, keepdims=True)
    whole = jnp.sum(counts * figures, axis=0, keepdims=True) / entries
    apart = jnp.sum(WIDTH * counts * jnp.square(figures - whole), axis=0, keepdims=True)
    within = jnp.sum(figures, axis=0, keepdims=True)
    out_row = lax.broadcasted_iota(jnp.int32, moments_ref.shape, 0)
    out_lane = lax.broadcasted_iota(jnp.int32, moments_ref.shape, 1)
    summary = jnp.zeros(moments_ref.shape, jnp.float32)
    means, scales = [], []
    for layer in range(LAYERS):
        at, beyond = 1 + layer, 1 + LAYERS + layer
        mean = whole[:, at : at + 1]
        variance = (apart[:, at : at + 1] + within[:, beyond : beyond + 1]) / (entries * WIDTH)
        means.append(mean)
        scales.append(lax.rsqrt(variance + epsilon))
        summary = jnp.where(out_lane == layer, jnp.where(out_row == 0, mean, variance), summary)
    moments_ref[...] = summary
    return means, scales


def normalize_kernel(order, used_ref, gain_ref, *refs):
    sources = refs[: -5]
    out_ref, moments_ref, figures_ref, ready_ref, sems = refs[-5:]
    _, slot_count, columns = out_ref.shape
    pieces = columns // LANES
    blocks = order(sources)
    for owner, block_ref, terms_ref in blocks:
        terms = (block_ref[pieces * slot_count :, :] if terms_ref is None else terms_ref[...]).astype(jnp.float32)
        figures_ref[pl.ds(owner, 1), :] = terms[0:1] + terms[1:2] + terms[2:3]
    means, scales = merge(figures_ref[...], moments_ref)
    slot = lax.broadcasted_iota(jnp.int32, (slot_count, LANES), 0)
    shift, factor = [], []
    for piece in range(pieces):
        layer = piece * LANES // WIDTH
        shift.append(jnp.broadcast_to(means[layer], (1, LANES)))
        factor.append(scales[layer] * gain_ref[:, piece * LANES : (piece + 1) * LANES])
    copies = []
    for place, (owner, block_ref, _) in enumerate(blocks):
        live = slot < used_ref[0, owner]
        for piece in range(pieces):
            x = block_ref[piece * slot_count : (piece + 1) * slot_count, :].astype(jnp.float32)
            ready_ref[place, :, piece * LANES : (piece + 1) * LANES] = jnp.where(
                live, (x - shift[piece]) * factor[piece], 0.0
            ).astype(jnp.bfloat16)
        copy = pltpu.make_async_copy(ready_ref.at[place], out_ref.at[owner], sems.at[place])
        copy.start()
        copies.append(copy)
    for copy in copies:
        copy.wait()


def normalize(order, request_counts, gain, sources, owners, slot_count):
    columns = gain.shape[0]
    return kernel_call(
        functools.partial(normalize_kernel, order),
        (
            jax.ShapeDtypeStruct((owners, slot_count, columns), jnp.bfloat16),
            jax.ShapeDtypeStruct((2, LAYERS), jnp.float32),
        ),
        [SMEM] + [VMEM] * (1 + len(sources)),
        (PLACED, VMEM),
        (
            pltpu.VMEM((owners, LANES), jnp.float32),
            pltpu.VMEM((owners, slot_count, columns), jnp.bfloat16),
            pltpu.SemaphoreType.DMA((owners,)),
        ),
    )(request_counts, gain[None], *sources)


def by_shift(shifts, early, sources):
    owners = len(shifts)
    me = lax.axis_index("rows")
    apart = list(sources[owners:]) + [None] * (owners - early)
    return [
        (lax.rem(me + owners - shift, owners), block_ref, terms_ref)
        for shift, block_ref, terms_ref in zip(shifts, sources[:owners], apart)
    ]


def by_owner(sources):
    (received_ref,) = sources
    return [(owner, received_ref.at[owner], None) for owner in range(received_ref.shape[0])]


def shifts_of(owners):
    return sorted(range(1, owners), key=lambda shift: (abs(shift - owners // 2), shift)) + [0]


def per_device(groups, requests, request_counts, table, gain):
    _, owners, slot_count = requests.shape
    held_rows, columns = table.shape
    pieces, blocks = columns // LANES, held_rows // LANES
    bare = jax.ShapeDtypeStruct((pieces * slot_count, LANES), jnp.bfloat16)
    message = jax.ShapeDtypeStruct((pieces * slot_count + SUBLANES, LANES), jnp.bfloat16)
    figures = jax.ShapeDtypeStruct((SUBLANES, LANES), jnp.bfloat16)
    counts = jax.ShapeDtypeStruct((blocks, LANES), jnp.int32)
    everywhere = (groups, owners, slot_count)
    slot = lax.broadcasted_iota(jnp.int32, everywhere, 2)
    outside = held_rows + lax.broadcasted_iota(jnp.int32, everywhere, 0)
    asked = jnp.where(slot < request_counts[0][None, :, None], requests[0][None], outside)
    wanted = lax.all_to_all(
        asked.reshape(groups * owners, slot_count), ("rep", "rows"), split_axis=0, concat_axis=0, tiled=True
    ).reshape(-1, LANES)
    moments = kernel_call(
        row_moments_kernel, jax.ShapeDtypeStruct((2 * LAYERS * blocks, LANES), jnp.float32), [VMEM], VMEM
    )(table)
    tally_scratch = (
        pltpu.VMEM((blocks, wanted.size), jnp.bfloat16),
        pltpu.VMEM((wanted.size, LANES), jnp.bfloat16),
    )
    if slot_count == LANES and owners <= MOST_PERMUTES // 2:
        shifts = shifts_of(owners)
        early = 1

        def send(a, shift):
            if not shift:
                return a
            return lax.ppermute(a, "rows", [(i, (i + shift) % owners) for i in range(owners)])

        wanted, *first = kernel_call(
            functools.partial(first_kernel, owners, shifts[:early]),
            (jax.ShapeDtypeStruct(wanted.shape, jnp.int32),) + (bare,) * early,
            [VMEM] * 2,
            (VMEM,) * (1 + early),
        )(wanted, table)
        sources = [send(a, shift) for a, shift in zip(first, shifts)]
        row_counts, terms = kernel_call(
            tally_kernel, (counts, figures), [VMEM] * 2, (VMEM,) * 2, tally_scratch
        )(wanted, moments)
        rest = kernel_call(
            functools.partial(serve_kernel, owners, shifts[early:]),
            (message,) * (owners - early),
            [VMEM] * 3,
            (VMEM,) * (owners - early),
        )(wanted, terms, table)
        sources += [send(a, shift) for a, shift in zip(rest, shifts[early:])]
        sources += [send(terms, shift) for shift in shifts[:early]]
        order = functools.partial(by_shift, shifts, early)
    else:
        mine = lax.dynamic_index_in_dim(
            wanted.reshape(groups, -1, LANES), lax.axis_index("rep"), 0, False
        )
        payload, row_counts = kernel_call(
            functools.partial(serve_all_kernel, slot_count),
            (jax.ShapeDtypeStruct((owners,) + message.shape, jnp.bfloat16), counts),
            [VMEM] * 4,
            (VMEM, VMEM),
            tally_scratch,
        )(mine, wanted, moments, table)
        sources = [lax.all_to_all(payload, "rows", split_axis=0, concat_axis=0, tiled=True)]
        order = by_owner
    normalized, summary = normalize(order, request_counts, gain, sources, owners, slot_count)
    return (normalized[None], row_counts.reshape(-1), summary)


def solution(mesh):
    return jax.shard_map(
        functools.partial(per_device, mesh.shape["rep"]),
        mesh=mesh,
        in_specs=(P(("rows", "rep"), None, None), P(("rows", "rep"), None), P("rows", None), P()),
        out_specs=(P(("rows", "rep"), None, None, None), P("rows"), P()),
        check_vma=False,
    )
```

profile of v0, /device:TPU:0, one launch (start us, length us, event | category | flops | bytes accessed | tf_op | source)
XLA Modules:
  0.0 50.1 jit_solution(9989273717966134967)
XLA Ops:
  0.6 0.1 iota.18
  0.7 0.1 iota.19
  0.8 0.0 copy-start.3
  0.8 0.0 copy-start.4
  0.8 0.7 %copy-done.3 = s32[1,8]{1,0:T(1,128)S(1)} copy-done((s32[1,8]{1,0:T(1,128)S(1)}, s32[1,8]{1,0:T(1,128)}, u32[]{:S(2)}) %copy-start.3) | copy-done | bytes 56
  1.5 0.1 lt.24
  1.5 0.0 copy-done.4
  1.5 0.7 %compare_select_fusion = s32[32,1,128]{2,1,0:T(1,128)} fusion(s32[32,1,128]{2,1,0:T(1,128)S(1)} %bitcast.10, s32[32]{0:T(128)S(1)} %iota.19, s32[32]{0:T(128)S(1)} %lt.24), kind=kLoop, calls=%fused_computation | loop fusion | flops 8192 | bytes 33024 | tf_op jit(solution)/shard_map/jit(_where)/select_n | solution.py:244
  2.3 7.3 %all-to-all-start = ((s32[32,1,128]{2,1,0:T(1,128)}), s32[32,1,128]{2,1,0:T(1,128)S(1)}, u32[]{:S(2)}, u32[]{:S(2)}) async-start(s32[32,1,128]{2,1,0:T(1,128)} %compare_select_fusion), calls=%async_computation | async-start | bytes 32768 | tf_op jit(solution)/shard_map/all_to_all | solution.py:245
  9.6 0.0 copy-start
  9.6 1.2 %copy-done = bf16[1024,512]{1,0:T(8,128)(2,1)S(1)} copy-done((bf16[1024,512]{1,0:T(8,128)(2,1)S(1)}, bf16[1024,512]{1,0:T(8,128)(2,1)}, u32[]{:S(2)}) %copy-start) | copy-done | bytes 1048600
  10.9 0.0 copy-start.1
  10.9 1.4 %shard_map.68.moments_ref = f32[32,128]{1,0:T(8,128)S(1)} custom-call(bf16[1024,512]{1,0:T(8,128)(2,1)S(1)} %copy-done), custom_call_target="tpu_custom_call" | custom-call | tf_op jit(solution)/shard_map/pallas_call | solution.py:248
  12.2 4.5 %all-to-all-done = s32[32,1,128]{2,1,0:T(1,128)S(1)} async-done(((s32[32,1,128]{2,1,0:T(1,128)}), s32[32,1,128]{2,1,0:T(1,128)S(1)}, u32[]{:S(2)}, u32[]{:S(2)}) %all-to-all-start) | async-done | bytes 16416 | tf_op jit(solution)/shard_map/all_to_all | solution.py:245
  16.7 0.0 copy-done.1
  16.7 0.4 shard_map.67
  17.1 1.7 %shard_map.69 = (s32[8,128]{1,0:T(8,128)}, bf16[8,128]{1,0:T(8,128)(2,1)S(1)}) custom-call(s32[32,128]{1,0:T(8,128)S(1)} %get-tuple-element.17.wanted_ref, f32[32,128]{1,0:T(8,128)S(1)} %shard_map.68.moments_ref), custom_call_target="tpu_custom_call" | custom-call | tf_op jit(solution)/shard_map/pallas_call | solution.py:271
  18.9 1.3 %shard_map.70 = (bf16[520,128]{1,0:T(8,128)(2,1)S(1)}, bf16[520,128]{1,0:T(8,128)(2,1)S(1)}, bf16[520,128]{1,0:T(8,128)(2,1)S(1)}, bf16[520,128]{1,0:T(8,128)(2,...) custom-call(s32[32,128]{1,0:T(8,128)S(1)} %get-tuple-element.17.wanted_ref, ...), custom_call_target="tpu_custom_call" | custom-call | tf_op jit(solution)/shard_map/pallas_call | solution.py:274
  20.1 0.7 %collective-permute-start.1 = (bf16[520,128]{1,0:T(8,128)(2,1)S(1)}, bf16[520,128]{1,0:T(8,128)(2,1)S(1)}, u32[]{:S(2)}, u32[]{:S(2)}) collective-permute-start(bf16[520,128]{1,0:T(8,128)(2,1)S(1)} %get-tuple-element.19), channel_id=1, source_target_pairs={{0,12},{4,16},{8,20},{12,24},{16,28},{20,0},{24,4},{28,8},{1,13},{... | collective-permute-start | bytes 399368 | tf_op jit(solution)/shard_map/ppermute | solution.py:262
  20.8 0.6 %collective-permute-start = (bf16[512,128]{1,0:T(8,128)(2,1)S(1)}, bf16[512,128]{1,0:T(8,128)(2,1)S(1)}, u32[]{:S(2)}, u32[]{:S(2)}) collective-permute-start(bf16[512,128]{1,0:T(8,128)(2,1)S(1)} %get-tuple-element.16), channel_id=1, source_target_pairs={{0,16},{4,20},{8,24},{12,28},{16,0},{20,4},{24,8},{28,12},{1,17},{... | collective-permute-start | bytes 393224 | tf_op jit(solution)/shard_map/ppermute | solution.py:262
  21.4 2.4 %collective-permute-start.7 = (bf16[8,128]{1,0:T(8,128)(2,1)S(1)}, bf16[8,128]{1,0:T(8,128)(2,1)S(1)}, u32[]{:S(2)}, u32[]{:S(2)}) collective-permute-start(bf16[8,128]{1,0:T(8,128)(2,1)S(1)} %get-tuple-element.18.terms_ref), channel_id=1, source_target_pairs={{0,16},{4,20},{8,24},{12,28},{16,0},{20,4},{24,8},{28,12},{1,17},{... | collective-permute-start | bytes 6152 | tf_op jit(solution)/shard_map/ppermute | solution.py:262
  23.7 3.2 %collective-permute-start.2 = (bf16[520,128]{1,0:T(8,128)(2,1)S(1)}, bf16[520,128]{1,0:T(8,128)(2,1)S(1)}, u32[]{:S(2)}, u32[]{:S(2)}) collective-permute-start(bf16[520,128]{1,0:T(8,128)(2,1)S(1)} %get-tuple-element.20), channel_id=1, source_target_pairs={{0,20},{4,24},{8,28},{12,0},{16,4},{20,8},{24,12},{28,16},{1,21},{... | collective-permute-start | bytes 399368 | tf_op jit(solution)/shard_map/ppermute | solution.py:262
  26.9 0.5 %collective-permute-start.3 = (bf16[520,128]{1,0:T(8,128)(2,1)S(1)}, bf16[520,128]{1,0:T(8,128)(2,1)S(1)}, u32[]{:S(2)}, u32[]{:S(2)}) collective-permute-start(bf16[520,128]{1,0:T(8,128)(2,1)S(1)} %get-tuple-element.21), channel_id=1, source_target_pairs={{0,8},{4,12},{8,16},{12,20},{16,24},{20,28},{24,0},{28,4},{1,9},{5... | collective-permute-start | bytes 399368 | tf_op jit(solution)/shard_map/ppermute | solution.py:262
  27.5 11.4 %collective-permute-done.7.refs_8_ = bf16[8,128]{1,0:T(8,128)(2,1)S(1)} collective-permute-done((bf16[8,128]{1,0:T(8,128)(2,1)S(1)}, bf16[8,128]{1,0:T(8,128)(2,1)S(1)}, u32[]{:S(2)}, u32[]{:S(2)}) %collective-permute-start.7) | collective-permute-done | bytes 2080 | tf_op jit(solution)/shard_map/ppermute | solution.py:262
  38.8 0.0 collective-permute-start.4
  38.8 0.0 collective-permute-done.refs_0_
  38.8 2.1 %collective-permute-start.5 = (bf16[520,128]{1,0:T(8,128)(2,1)S(1)}, bf16[520,128]{1,0:T(8,128)(2,1)S(1)}, u32[]{:S(2)}, u32[]{:S(2)}) collective-permute-start(bf16[520,128]{1,0:T(8,128)(2,1)S(1)} %get-tuple-element.23), channel_id=1, source_target_pairs={{0,4},{4,8},{8,12},{12,16},{16,20},{20,24},{24,28},{28,0},{1,5},{5... | collective-permute-start | bytes 399368 | tf_op jit(solution)/shard_map/ppermute | solution.py:262
  40.9 0.0 collective-permute-done.1.refs_1_
  40.9 0.0 copy-start.2
  40.9 2.6 %collective-permute-start.6 = (bf16[520,128]{1,0:T(8,128)(2,1)S(1)}, bf16[520,128]{1,0:T(8,128)(2,1)S(1)}, u32[]{:S(2)}, u32[]{:S(2)}) collective-permute-start(bf16[520,128]{1,0:T(8,128)(2,1)S(1)} %get-tuple-element.24), channel_id=1, source_target_pairs={{0,28},{4,0},{8,4},{12,8},{16,12},{20,16},{24,20},{28,24},{1,29},{... | collective-permute-start | bytes 399368 | tf_op jit(solution)/shard_map/ppermute | solution.py:262
  43.6 0.0 collective-permute-done.2.refs_2_
  43.6 0.0 collective-permute-done.3.refs_3_
  43.6 1.6 %collective-permute-done.4.refs_4_ = bf16[520,128]{1,0:T(8,128)(2,1)S(1)} collective-permute-done((bf16[520,128]{1,0:T(8,128)(2,1)S(1)}, bf16[520,128]{1,0:T(8,128)(2,1)S(1)}, u32[]{:S(2)}, u32[]{:S(2)}) %collective-permute-start.4) | collective-permute-done | bytes 133152 | tf_op jit(solution)/shard_map/ppermute | solution.py:262
  45.2 1.4 %collective-permute-done.5.refs_5_ = bf16[520,128]{1,0:T(8,128)(2,1)S(1)} collective-permute-done((bf16[520,128]{1,0:T(8,128)(2,1)S(1)}, bf16[520,128]{1,0:T(8,128)(2,1)S(1)}, u32[]{:S(2)}, u32[]{:S(2)}) %collective-permute-start.5) | collective-permute-done | bytes 133152 | tf_op jit(solution)/shard_map/ppermute | solution.py:262
  46.5 1.2 %collective-permute-done.6.refs_6_ = bf16[520,128]{1,0:T(8,128)(2,1)S(1)} collective-permute-done((bf16[520,128]{1,0:T(8,128)(2,1)S(1)}, bf16[520,128]{1,0:T(8,128)(2,1)S(1)}, u32[]{:S(2)}, u32[]{:S(2)}) %collective-permute-start.6) | collective-permute-done | bytes 133152 | tf_op jit(solution)/shard_map/ppermute | solution.py:262
  47.7 0.0 copy-done.2
  47.7 2.4 %shard_map.71 = (bf16[8,128,512]{2,1,0:T(8,128)(2,1)}, f32[2,2]{1,0:T(2,128)}) custom-call(s32[1,8]{1,0:T(1,128)S(1)} %copy-done.3, f32[1,512]{1,0:T(1,128)S(1)} %bitcast.8, bf16[512,128]{1,0:T(8,128)(2,1)S(1)} %collective-permute-done.refs_0_, bf16[520,128]{1,0:T(8,128)(2,1)S(1)} %collective-permute-done.1.refs_1_, ...), custom_call_target="tpu_custom_call" | custom-call | tf_op jit(solution)/shard_map/pallas_call | solution.py:198
  (3 shorter events, 0.0 us)
Async XLA Ops:
  0.8 0.7 %copy-start.3 = (s32[1,8]{1,0:T(1,128)S(1)}, s32[1,8]{1,0:T(1,128)}, u32[]{:S(2)}) copy-start(s32[1,8]{1,0:T(1,128)} %used_ref.1) | copy-start | bytes 100
  0.8 0.7 %copy-start.4 = (s32[1,8,128]{2,1,0:T(8,128)S(1)}, s32[1,8,128]{2,1,0:T(8,128)}, u32[]{:S(2)}) copy-start(s32[1,8,128]{2,1,0:T(8,128)} %param.4) | copy-start | bytes 12292
  2.3 14.4 %all-to-all-start = ((s32[32,1,128]{2,1,0:T(1,128)}), s32[32,1,128]{2,1,0:T(1,128)S(1)}, u32[]{:S(2)}, u32[]{:S(2)}) async-start(s32[32,1,128]{2,1,0:T(1,128)} %compare_select_fusion), calls=%async_computation | async-start | bytes 32768 | tf_op jit(solution)/shard_map/all_to_all | solution.py:245
  9.6 1.2 %copy-start = (bf16[1024,512]{1,0:T(8,128)(2,1)S(1)}, bf16[1024,512]{1,0:T(8,128)(2,1)}, u32[]{:S(2)}) copy-start(bf16[1024,512]{1,0:T(8,128)(2,1)} %table_ref.5) | copy-start | bytes 3145732
  10.9 5.8 %copy-start.1 = (bf16[1024,512]{1,0:T(8,128)(2,1)S(1)}, bf16[1024,512]{1,0:T(8,128)(2,1)}, u32[]{:S(2)}) copy-start(bf16[1024,512]{1,0:T(8,128)(2,1)} %table_ref.5) | copy-start | bytes 3145732
  20.1 20.8 %collective-permute-start.1 = (bf16[520,128]{1,0:T(8,128)(2,1)S(1)}, bf16[520,128]{1,0:T(8,128)(2,1)S(1)}, u32[]{:S(2)}, u32[]{:S(2)}) collective-permute-start(bf16[520,128]{1,0:T(8,128)(2,1)S(1)} %get-tuple-element.19), channel_id=1, source_target_pairs={{0,12},{4,16},{8,20},{12,24},{16,28},{20,0},{24,4},{28,8},{1,13},{... | collective-permute-start | bytes 399368 | tf_op jit(solution)/shard_map/ppermute | solution.py:262
  20.8 18.0 %collective-permute-start = (bf16[512,128]{1,0:T(8,128)(2,1)S(1)}, bf16[512,128]{1,0:T(8,128)(2,1)S(1)}, u32[]{:S(2)}, u32[]{:S(2)}) collective-permute-start(bf16[512,128]{1,0:T(8,128)(2,1)S(1)} %get-tuple-element.16), channel_id=1, source_target_pairs={{0,16},{4,20},{8,24},{12,28},{16,0},{20,4},{24,8},{28,12},{1,17},{... | collective-permute-start | bytes 393224 | tf_op jit(solution)/shard_map/ppermute | solution.py:262
  21.4 17.4 %collective-permute-start.7 = (bf16[8,128]{1,0:T(8,128)(2,1)S(1)}, bf16[8,128]{1,0:T(8,128)(2,1)S(1)}, u32[]{:S(2)}, u32[]{:S(2)}) collective-permute-start(bf16[8,128]{1,0:T(8,128)(2,1)S(1)} %get-tuple-element.18.terms_ref), channel_id=1, source_target_pairs={{0,16},{4,20},{8,24},{12,28},{16,0},{20,4},{24,8},{28,12},{1,17},{... | collective-permute-start | bytes 6152 | tf_op jit(solution)/shard_map/ppermute | solution.py:262
  23.7 19.8 %collective-permute-start.2 = (bf16[520,128]{1,0:T(8,128)(2,1)S(1)}, bf16[520,128]{1,0:T(8,128)(2,1)S(1)}, u32[]{:S(2)}, u32[]{:S(2)}) collective-permute-start(bf16[520,128]{1,0:T(8,128)(2,1)S(1)} %get-tuple-element.20), channel_id=1, source_target_pairs={{0,20},{4,24},{8,28},{12,0},{16,4},{20,8},{24,12},{28,16},{1,21},{... | collective-permute-start | bytes 399368 | tf_op jit(solution)/shard_map/ppermute | solution.py:262
  26.9 16.6 %collective-permute-start.3 = (bf16[520,128]{1,0:T(8,128)(2,1)S(1)}, bf16[520,128]{1,0:T(8,128)(2,1)S(1)}, u32[]{:S(2)}, u32[]{:S(2)}) collective-permute-start(bf16[520,128]{1,0:T(8,128)(2,1)S(1)} %get-tuple-element.21), channel_id=1, source_target_pairs={{0,8},{4,12},{8,16},{12,20},{16,24},{20,28},{24,0},{28,4},{1,9},{5... | collective-permute-start | bytes 399368 | tf_op jit(solution)/shard_map/ppermute | solution.py:262
  38.8 6.3 %collective-permute-start.4 = (bf16[520,128]{1,0:T(8,128)(2,1)S(1)}, bf16[520,128]{1,0:T(8,128)(2,1)S(1)}, u32[]{:S(2)}, u32[]{:S(2)}) collective-permute-start(bf16[520,128]{1,0:T(8,128)(2,1)S(1)} %get-tuple-element.22), channel_id=1, source_target_pairs={{0,24},{4,28},{8,0},{12,4},{16,8},{20,12},{24,16},{28,20},{1,25},{... | collective-permute-start | bytes 399368 | tf_op jit(solution)/shard_map/ppermute | solution.py:262
  38.8 7.7 %collective-permute-start.5 = (bf16[520,128]{1,0:T(8,128)(2,1)S(1)}, bf16[520,128]{1,0:T(8,128)(2,1)S(1)}, u32[]{:S(2)}, u32[]{:S(2)}) collective-permute-start(bf16[520,128]{1,0:T(8,128)(2,1)S(1)} %get-tuple-element.23), channel_id=1, source_target_pairs={{0,4},{4,8},{8,12},{12,16},{16,20},{20,24},{24,28},{28,0},{1,5},{5... | collective-permute-start | bytes 399368 | tf_op jit(solution)/shard_map/ppermute | solution.py:262
  40.9 6.8 %copy-start.2 = (f32[512]{0:T(512)S(1)}, f32[512]{0:T(512)}, u32[]{:S(2)}) copy-start(f32[512]{0:T(512)} %param.7) | copy-start | bytes 6148
  40.9 6.8 %collective-permute-start.6 = (bf16[520,128]{1,0:T(8,128)(2,1)S(1)}, bf16[520,128]{1,0:T(8,128)(2,1)S(1)}, u32[]{:S(2)}, u32[]{:S(2)}) collective-permute-start(bf16[520,128]{1,0:T(8,128)(2,1)S(1)} %get-tuple-element.24), channel_id=1, source_target_pairs={{0,28},{4,0},{8,4},{12,8},{16,12},{20,16},{24,20},{28,24},{1,29},{... | collective-permute-start | bytes 399368 | tf_op jit(solution)/shard_map/ppermute | solution.py:262
where the time goes:
time: 50.3 us; the launch traced here: 50.1 us
  waiting for transfers between devices  20 us (40%)
  starting transfers between devices  19.4 us (39%)
  Pallas kernels  7.2 us (14%)
  local copies, waits for them, and re-layouts  2.13 us (4%)
  other arithmetic  0.75 us (1%)
  between operations  0.69 us (1%)
    ppermute x8, waiting for transfers between devices, send(): lax.ppermute(a, 'rows', [(i, (i + shift) % owners) for i in range(owners)])  15.5 us
    ppermute x8, starting transfers between devices, send(): lax.ppermute(a, 'rows', [(i, (i + shift) % owners) for i in range(owners)])  12.1 us
    all_to_all x1, starting transfers between devices, per_device(): lax.all_to_all(asked.reshape(groups * owners, slot_count), ('rep', 'rows'...  7.33 us
    all_to_all x1, waiting for transfers between devices, per_device(): lax.all_to_all(asked.reshape(groups * owners, slot_count), ('rep', 'rows'...  4.47 us
    pallas_call x1, Pallas kernels, normalize(): kernel_call(functools.partial(normalize_kernel, order), (jax.ShapeDtypeSt...  2.4 us
    unnamed x10, local copies, waits for them, and re-layouts  1.89 us
    pallas_call x1, Pallas kernels, per_device(): kernel_call(tally_kernel, (counts, figures), [VMEM] * 2, (VMEM,) * 2, tal...  1.72 us
    pallas_call x1, Pallas kernels, per_device(): kernel_call(row_moments_kernel, jax.ShapeDtypeStruct((2 * LAYERS * blocks...  1.37 us
  transfers between devices with their start and end apart: 9, of which 5 were waited for; matrix products, arithmetic and copies ran while one was open for 0% of the time, Pallas kernels for 3%

commit v1 on v0

--- a/solution.py
+++ b/solution.py
@@ -13,14 +13,15 @@
 LANES = 128
 SUBLANES = 8
 GRANT = 16 << 20
+WIDE_GRANT = 60 << 20
 MOST_PERMUTES = 16
 
 epsilon = 1e-06
 
 
 VMEM = pl.BlockSpec(memory_space=pltpu.VMEM)
-SMEM = pl.BlockSpec(memory_space=pltpu.SMEM)
 PLACED = pl.BlockSpec(memory_space=pl.ANY)
+HBM = pl.BlockSpec(memory_space=pltpu.HBM)
 
 
 def total(a):
@@ -31,18 +32,19 @@
     return jnp.where(match, 1.0, 0.0).astype(jnp.bfloat16)
 
 
-def kernel_call(body, out_shape, in_specs, out_specs, scratch=()):
+def kernel_call(body, out_shape, in_specs, out_specs, scratch=(), grant=GRANT):
     return pl.pallas_call(
         body,
         out_shape=out_shape,
         in_specs=in_specs,
         out_specs=out_specs,
         scratch_shapes=list(scratch),
-        compiler_params=pltpu.CompilerParams(vmem_limit_bytes=GRANT),
+        compiler_params=pltpu.CompilerParams(vmem_limit_bytes=grant),
     )
 
 
-def row_moments_kernel(table_ref, moments_ref):
+def row_moments_kernel(table_ref, gain_ref, moments_ref, kept_gain_ref):
+    kept_gain_ref[...] = gain_ref[...]
     blocks = table_ref.shape[0] // LANES
     lane = lax.broadcasted_iota(jnp.int32, (LANES, LANES), 1)
     columns = jnp.zeros((LANES, LANES), jnp.float32)
@@ -56,6 +58,30 @@
             columns = jnp.where(lane == layer * blocks + block, mean, columns)
             columns = jnp.where(lane == (LAYERS + layer) * blocks + block, square, columns)
     moments_ref[...] = jnp.transpose(columns)[: 2 * LAYERS * blocks]
+
+
+def ask_kernel(held_rows, used_hbm, requests_hbm, everywhere_hbm, used_ref, requests_ref, asked_ref, sems):
+    owners, slot_count = requests_ref.shape
+    copies = [
+        pltpu.make_async_copy(used_hbm, used_ref, sems.at[0]),
+        pltpu.make_async_copy(requests_hbm, requests_ref, sems.at[1]),
+    ]
+    for copy in copies:
+        copy.start()
+    row = lax.broadcasted_iota(jnp.int32, (owners, slot_count), 0)
+    slot = lax.broadcasted_iota(jnp.int32, (owners, slot_count), 1)
+    copies[0].wait()
+    used = jnp.zeros((owners, slot_count), jnp.int32)
+    for owner in range(owners):
+        used = jnp.where(row == owner, used_ref[0, owner], used)
+    copies[1].wait()
+    asked_ref[...] = jnp.where(slot < used, requests_ref[...], held_rows)
+    copies = []
+    for group in range(everywhere_hbm.shape[0]):
+        copies.append(pltpu.make_async_copy(asked_ref, everywhere_hbm.at[group], sems.at[2 + group]))
+        copies[-1].start()
+    for copy in copies:
+        copy.wait()
 
 
 def tally(wanted, moments_ref, high_ref, low_ref, counts_ref):
@@ -162,53 +188,59 @@
     return means, scales
 
 
-def normalize_kernel(order, used_ref, gain_ref, *refs):
-    sources = refs[: -5]
-    out_ref, moments_ref, figures_ref, ready_ref, sems = refs[-5:]
-    _, slot_count, columns = out_ref.shape
+def normalize_kernel(order, held_rows, asked_ref, gain_ref, tally_ref, *refs):
+    sources = refs[:-8]
+    out_ref, counts_ref, moments_ref, figures_ref, ready_ref, summary_ref, sems, other_sems = refs[-8:]
+    owners, slot_count, columns = out_ref.shape
     pieces = columns // LANES
+    copies = [pltpu.make_async_copy(tally_ref, counts_ref, other_sems.at[0])]
+    copies[0].start()
     blocks = order(sources)
     for owner, block_ref, terms_ref in blocks:
         terms = (block_ref[pieces * slot_count :, :] if terms_ref is None else terms_ref[...]).astype(jnp.float32)
         figures_ref[pl.ds(owner, 1), :] = terms[0:1] + terms[1:2] + terms[2:3]
-    means, scales = merge(figures_ref[...], moments_ref)
-    slot = lax.broadcasted_iota(jnp.int32, (slot_count, LANES), 0)
+    means, scales = merge(figures_ref[...], summary_ref)
+    copies.append(pltpu.make_async_copy(summary_ref, moments_ref, other_sems.at[1]))
+    copies[1].start()
+    asked = [asked_ref[pl.ds(owner, 1), :] for owner, _, _ in blocks]
+    asked = jnp.transpose(jnp.concatenate(asked + asked[:1] * (-owners % SUBLANES), axis=0))
     shift, factor = [], []
     for piece in range(pieces):
         layer = piece * LANES // WIDTH
         shift.append(jnp.broadcast_to(means[layer], (1, LANES)))
         factor.append(scales[layer] * gain_ref[:, piece * LANES : (piece + 1) * LANES])
-    copies = []
     for place, (owner, block_ref, _) in enumerate(blocks):
-        live = slot < used_ref[0, owner]
+        live = asked[:, place : place + 1] < held_rows
         for piece in range(pieces):
             x = block_ref[piece * slot_count : (piece + 1) * slot_count, :].astype(jnp.float32)
             ready_ref[place, :, piece * LANES : (piece + 1) * LANES] = jnp.where(
                 live, (x - shift[piece]) * factor[piece], 0.0
             ).astype(jnp.bfloat16)
-        copy = pltpu.make_async_copy(ready_ref.at[place], out_ref.at[owner], sems.at[place])
-        copy.start()
-        copies.append(copy)
+        copies.append(pltpu.make_async_copy(ready_ref.at[place], out_ref.at[owner], sems.at[place]))
+        copies[-1].start()
     for copy in copies:
         copy.wait()
 
 
-def normalize(order, request_counts, gain, sources, owners, slot_count):
-    columns = gain.shape[0]
+def normalize(order, held_rows, asked, gain, tallied, sources):
+    (owners, slot_count), columns = asked.shape, gain.shape[1]
     return kernel_call(
-        functools.partial(normalize_kernel, order),
+        functools.partial(normalize_kernel, order, held_rows),
         (
             jax.ShapeDtypeStruct((owners, slot_count, columns), jnp.bfloat16),
+            jax.ShapeDtypeStruct(tallied.shape, jnp.int32),
             jax.ShapeDtypeStruct((2, LAYERS), jnp.float32),
         ),
-        [SMEM] + [VMEM] * (1 + len(sources)),
-        (PLACED, VMEM),
+        [VMEM] * (3 + len(sources)),
+        (PLACED,) * 3,
         (
             pltpu.VMEM((owners, LANES), jnp.float32),
             pltpu.VMEM((owners, slot_count, columns), jnp.bfloat16),
+            pltpu.VMEM((2, LAYERS), jnp.float32),
             pltpu.SemaphoreType.DMA((owners,)),
+            pltpu.SemaphoreType.DMA((2,)),
         ),
-    )(request_counts, gain[None], *sources)
+    )(asked, gain, tallied, *sources)
 
 
 def by_shift(shifts, early, sources):
@@ -238,21 +270,43 @@
     message = jax.ShapeDtypeStruct((pieces * slot_count + SUBLANES, LANES), jnp.bfloat16)
     figures = jax.ShapeDtypeStruct((SUBLANES, LANES), jnp.bfloat16)
     counts = jax.ShapeDtypeStruct((blocks, LANES), jnp.int32)
-    everywhere = (groups, owners, slot_count)
-    slot = lax.broadcasted_iota(jnp.int32, everywhere, 2)
-    outside = held_rows + lax.broadcasted_iota(jnp.int32, everywhere, 0)
-    asked = jnp.where(slot < request_counts[0][None, :, None], requests[0][None], outside)
+    by_permutes = slot_count == LANES and owners <= MOST_PERMUTES // 2
+    if by_permutes:
+        everywhere = kernel_call(
+            functools.partial(ask_kernel, held_rows),
+            jax.ShapeDtypeStruct((groups, owners, slot_count), jnp.int32),
+            [HBM] * 2,
+            HBM,
+            (
+                pltpu.SMEM((1, owners), jnp.int32),
+                pltpu.VMEM((owners, slot_count), jnp.int32),
+                pltpu.VMEM((owners, slot_count), jnp.int32),
+                pltpu.SemaphoreType.DMA((2 + groups,)),
+            ),
+            WIDE_GRANT,
+        )(request_counts, requests[0])
+        asked = everywhere[0]
+    else:
+        slot = lax.broadcasted_iota(jnp.int32, (owners, slot_count), 1)
+        asked = jnp.where(slot < request_counts[0][:, None], requests[0], held_rows)
+        everywhere = jnp.broadcast_to(asked[None], (groups, owners, slot_count))
     wanted = lax.all_to_all(
-        asked.reshape(groups * owners, slot_count), ("rep", "rows"), split_axis=0, concat_axis=0, tiled=True
+        everywhere.reshape(groups * owners, slot_count), ("rep", "rows"), split_axis=0, concat_axis=0, tiled=True
     ).reshape(-1, LANES)
-    moments = kernel_call(
-        row_moments_kernel, jax.ShapeDtypeStruct((2 * LAYERS * blocks, LANES), jnp.float32), [VMEM], VMEM
-    )(table)
+    moments, gain = kernel_call(
+        row_moments_kernel,
+        (
+            jax.ShapeDtypeStruct((2 * LAYERS * blocks, LANES), jnp.float32),
+            jax.ShapeDtypeStruct((1, columns), jnp.float32),
+        ),
+        [VMEM] * 2,
+        (VMEM,) * 2,
+    )(table, gain[None])
     tally_scratch = (
         pltpu.VMEM((blocks, wanted.size), jnp.bfloat16),
         pltpu.VMEM((wanted.size, LANES), jnp.bfloat16),
     )
-    if slot_count == LANES and owners <= MOST_PERMUTES // 2:
+    if by_permutes:
         shifts = shifts_of(owners)
         early = 1
 
@@ -268,7 +322,7 @@
             (VMEM,) * (1 + early),
         )(wanted, table)
         sources = [send(a, shift) for a, shift in zip(first, shifts)]
-        row_counts, terms = kernel_call(
+        tallied, terms = kernel_call(
             tally_kernel, (counts, figures), [VMEM] * 2, (VMEM,) * 2, tally_scratch
         )(wanted, moments)
         rest = kernel_call(
@@ -284,7 +338,7 @@
         mine = lax.dynamic_index_in_dim(
             wanted.reshape(groups, -1, LANES), lax.axis_index("rep"), 0, False
         )
-        payload, row_counts = kernel_call(
+        payload, tallied = kernel_call(
             functools.partial(serve_all_kernel, slot_count),
             (jax.ShapeDtypeStruct((owners,) + message.shape, jnp.bfloat16), counts),
             [VMEM] * 4,
@@ -293,7 +347,7 @@
         )(mine, wanted, moments, table)
         sources = [lax.all_to_all(payload, "rows", split_axis=0, concat_axis=0, tiled=True)]
         order = by_owner
-    normalized, summary = normalize(order, request_counts, gain, sources, owners, slot_count)
+    normalized, row_counts, summary = normalize(order, held_rows, asked, gain, tallied, sources)
     return (normalized[None], row_counts.reshape(-1), summary)
 
 

time: 50.3 us -> 48.8 us (0.970)
  other arithmetic: 0.75 us -> 0 us
  waiting for transfers between devices: 20 us -> 19.3 us
    select_n x1 -> x0, other arithmetic: 0.74 us -> none  [per_device(): jnp.where(slot < request_counts[0][None, :, None], requests[0][None], out...]
    ppermute x8, waiting for transfers between devices: 15.5 us -> 14.8 us  [send(): lax.ppermute(a, 'rows', [(i, (i + shift) % owners) for i in range(owners)])]
    squeeze x0 -> x1, local copies, waits for them, and re-layouts: none -> 0.69 us  [per_device(): asked = everywhere[0]]
    unnamed x10 -> x6, local copies, waits for them, and re-layouts: 1.89 us -> 1.23 us
    pallas_call x2 -> x3, Pallas kernels: 3.77 us -> 4.27 us  [the longest x1 1.55 us: normalize(): kernel_call(functools.partial(normalize_kernel, order, held_rows), (jax.S...]
  transfers between devices with their start and end apart: 9 -> 9, of which waited for: 5 -> 5; matrix products, arithmetic and copies ran while one was open for 0% -> 1% of each run, Pallas kernels for 3% -> 3%
where the time goes in v1:
time: 48.8 us; the launch traced here: 48.6 us
  starting transfers between devices  19.4 us (40%)
  waiting for transfers between devices  19.3 us (40%)
  Pallas kernels  7.28 us (15%)
  local copies, waits for them, and re-layouts  1.92 us (4%)
  between operations  0.7 us (1%)
    ppermute x8, waiting for transfers between devices, send(): lax.ppermute(a, 'rows', [(i, (i + shift) % owners) for i in range(owners)])  14.8 us
    ppermute x8, starting transfers between devices, send(): lax.ppermute(a, 'rows', [(i, (i + shift) % owners) for i in range(owners)])  12.1 us
    all_to_all x1, starting transfers between devices, per_device(): lax.all_to_all(everywhere.reshape(groups * owners, slot_count), ('rep', '...  7.33 us
    all_to_all x1, waiting for transfers between devices, per_device(): lax.all_to_all(everywhere.reshape(groups * owners, slot_count), ('rep', '...  4.46 us
    pallas_call x1, Pallas kernels, normalize(): kernel_call(functools.partial(normalize_kernel, order, held_rows), (jax.S...  1.55 us
    pallas_call x1, Pallas kernels, per_device(): kernel_call(row_moments_kernel, (jax.ShapeDtypeStruct((2 * LAYERS * block...  1.37 us
    pallas_call x1, Pallas kernels, per_device(): kernel_call(functools.partial(ask_kernel, held_rows), jax.ShapeDtypeStruc...  1.34 us
    pallas_call x1, Pallas kernels, per_device(): kernel_call(tally_kernel, (counts, figures), [VMEM] * 2, (VMEM,) * 2, tal...  1.31 us
  transfers between devices with their start and end apart: 9, of which 5 were waited for; matrix products, arithmetic and copies ran while one was open for 1% of the time, Pallas kernels for 3%

profile of v1, /device:TPU:0, one launch (start us, length us, event | category | flops | bytes accessed | tf_op | source)
XLA Modules:
  0.0 48.6 jit_solution(10671336907882926302)
XLA Ops:
  0.6 1.3 %shard_map.67 = s32[4,8,128]{2,1,0:T(8,128)} custom-call(s32[1,8]{1,0:T(1,128)} %used_hbm.1, s32[8,128]{1,0:T(8,128)} %bitcast.13), custom_call_target="tpu_custom_call" | custom-call | tf_op jit(solution)/shard_map/pallas_call | solution.py:275
  2.0 0.0 copy-start.2
  2.0 7.3 %all-to-all-start = ((s32[32,1,128]{2,1,0:T(1,128)}), s32[32,1,128]{2,1,0:T(1,128)S(1)}, u32[]{:S(2)}, u32[]{:S(2)}) async-start(s32[32,1,128]{2,1,0:T(1,128)} %bitcast.12), calls=%async_computation | async-start | bytes 32768 | tf_op jit(solution)/shard_map/all_to_all | solution.py:293
  9.3 0.0 copy-done.2
  9.3 0.0 copy-start
  9.4 1.2 %copy-done = bf16[1024,512]{1,0:T(8,128)(2,1)S(1)} copy-done((bf16[1024,512]{1,0:T(8,128)(2,1)S(1)}, bf16[1024,512]{1,0:T(8,128)(2,1)}, u32[]{:S(2)}) %copy-start) | copy-done | bytes 1048600
  10.6 0.0 copy-start.1
  10.6 1.4 %shard_map.68 = (f32[32,128]{1,0:T(8,128)S(1)}, f32[1,512]{1,0:T(1,128)S(1)}) custom-call(bf16[1024,512]{1,0:T(8,128)(2,1)S(1)} %copy-done, f32[1,512]{1,0:T(1,128)S(1)} %bitcast.11), custom_call_target="tpu_custom_call" | custom-call | tf_op jit(solution)/shard_map/pallas_call | solution.py:296
  11.9 4.5 %all-to-all-done = s32[32,1,128]{2,1,0:T(1,128)S(1)} async-done(((s32[32,1,128]{2,1,0:T(1,128)}), s32[32,1,128]{2,1,0:T(1,128)S(1)}, u32[]{:S(2)}, u32[]{:S(2)}) %all-to-all-start) | async-done | bytes 16416 | tf_op jit(solution)/shard_map/all_to_all | solution.py:293
  16.4 0.0 copy-done.1
  16.4 0.4 shard_map.69
  16.9 1.3 %shard_map.70 = (s32[8,128]{1,0:T(8,128)S(1)}, bf16[8,128]{1,0:T(8,128)(2,1)S(1)}) custom-call(s32[32,128]{1,0:T(8,128)S(1)} %get-tuple-element.20.wanted_ref, f32[32,128]{1,0:T(8,128)S(1)} %get-tuple-element.21.moments_ref), custom_call_target="tpu_custom_call" | custom-call | tf_op jit(solution)/shard_map/pallas_call | solution.py:325
  18.2 1.3 %shard_map.71 = (bf16[520,128]{1,0:T(8,128)(2,1)S(1)}, bf16[520,128]{1,0:T(8,128)(2,1)S(1)}, bf16[520,128]{1,0:T(8,128)(2,1)S(1)}, bf16[520,128]{1,0:T(8,128)(2,...) custom-call(s32[32,128]{1,0:T(8,128)S(1)} %get-tuple-element.20.wanted_ref, ...), custom_call_target="tpu_custom_call" | custom-call | tf_op jit(solution)/shard_map/pallas_call | solution.py:328
  19.4 0.7 %collective-permute-start.1 = (bf16[520,128]{1,0:T(8,128)(2,1)S(1)}, bf16[520,128]{1,0:T(8,128)(2,1)S(1)}, u32[]{:S(2)}, u32[]{:S(2)}) collective-permute-start(bf16[520,128]{1,0:T(8,128)(2,1)S(1)} %get-tuple-element.25), channel_id=1, source_target_pairs={{0,12},{4,16},{8,20},{12,24},{16,28},{20,0},{24,4},{28,8},{1,13},{... | collective-permute-start | bytes 399368 | tf_op jit(solution)/shard_map/ppermute | solution.py:316
  20.1 0.6 %collective-permute-start = (bf16[512,128]{1,0:T(8,128)(2,1)S(1)}, bf16[512,128]{1,0:T(8,128)(2,1)S(1)}, u32[]{:S(2)}, u32[]{:S(2)}) collective-permute-start(bf16[512,128]{1,0:T(8,128)(2,1)S(1)} %get-tuple-element.23), channel_id=1, source_target_pairs={{0,16},{4,20},{8,24},{12,28},{16,0},{20,4},{24,8},{28,12},{1,17},{... | collective-permute-start | bytes 393224 | tf_op jit(solution)/shard_map/ppermute | solution.py:316
  20.7 2.3 %collective-permute-start.7 = (bf16[8,128]{1,0:T(8,128)(2,1)S(1)}, bf16[8,128]{1,0:T(8,128)(2,1)S(1)}, u32[]{:S(2)}, u32[]{:S(2)}) collective-permute-start(bf16[8,128]{1,0:T(8,128)(2,1)S(1)} %get-tuple-element.24.terms_ref), channel_id=1, source_target_pairs={{0,16},{4,20},{8,24},{12,28},{16,0},{20,4},{24,8},{28,12},{1,17},{... | collective-permute-start | bytes 6152 | tf_op jit(solution)/shard_map/ppermute | solution.py:316
  23.0 3.2 %collective-permute-start.2 = (bf16[520,128]{1,0:T(8,128)(2,1)S(1)}, bf16[520,128]{1,0:T(8,128)(2,1)S(1)}, u32[]{:S(2)}, u32[]{:S(2)}) collective-permute-start(bf16[520,128]{1,0:T(8,128)(2,1)S(1)} %get-tuple-element.26), channel_id=1, source_target_pairs={{0,20},{4,24},{8,28},{12,0},{16,4},{20,8},{24,12},{28,16},{1,21},{... | collective-permute-start | bytes 399368 | tf_op jit(solution)/shard_map/ppermute | solution.py:316
  26.2 0.5 %collective-permute-start.3 = (bf16[520,128]{1,0:T(8,128)(2,1)S(1)}, bf16[520,128]{1,0:T(8,128)(2,1)S(1)}, u32[]{:S(2)}, u32[]{:S(2)}) collective-permute-start(bf16[520,128]{1,0:T(8,128)(2,1)S(1)} %get-tuple-element.27), channel_id=1, source_target_pairs={{0,8},{4,12},{8,16},{12,20},{16,24},{20,28},{24,0},{28,4},{1,9},{5... | collective-permute-start | bytes 399368 | tf_op jit(solution)/shard_map/ppermute | solution.py:316
  26.8 11.4 %collective-permute-done.7.refs_8_ = bf16[8,128]{1,0:T(8,128)(2,1)S(1)} collective-permute-done((bf16[8,128]{1,0:T(8,128)(2,1)S(1)}, bf16[8,128]{1,0:T(8,128)(2,1)S(1)}, u32[]{:S(2)}, u32[]{:S(2)}) %collective-permute-start.7) | collective-permute-done | bytes 2080 | tf_op jit(solution)/shard_map/ppermute | solution.py:316
  38.1 0.0 collective-permute-start.4
  38.1 0.0 collective-permute-done.refs_0_
  38.1 2.1 %collective-permute-start.5 = (bf16[520,128]{1,0:T(8,128)(2,1)S(1)}, bf16[520,128]{1,0:T(8,128)(2,1)S(1)}, u32[]{:S(2)}, u32[]{:S(2)}) collective-permute-start(bf16[520,128]{1,0:T(8,128)(2,1)S(1)} %get-tuple-element.29), channel_id=1, source_target_pairs={{0,4},{4,8},{8,12},{12,16},{16,20},{20,24},{24,28},{28,0},{1,5},{5... | collective-permute-start | bytes 399368 | tf_op jit(solution)/shard_map/ppermute | solution.py:316
  40.2 0.0 collective-permute-done.1.refs_1_
  40.2 2.6 %collective-permute-start.6 = (bf16[520,128]{1,0:T(8,128)(2,1)S(1)}, bf16[520,128]{1,0:T(8,128)(2,1)S(1)}, u32[]{:S(2)}, u32[]{:S(2)}) collective-permute-start(bf16[520,128]{1,0:T(8,128)(2,1)S(1)} %get-tuple-element.30), channel_id=1, source_target_pairs={{0,28},{4,0},{8,4},{12,8},{16,12},{20,16},{24,20},{28,24},{1,29},{... | collective-permute-start | bytes 399368 | tf_op jit(solution)/shard_map/ppermute | solution.py:316
  42.9 0.7 %slice_bitcast_fusion.asked_ref = s32[8,128]{1,0:T(8,128)S(1)} fusion(s32[4,8,128]{2,1,0:T(8,128)} %shard_map.67), kind=kLoop, calls=%fused_computation | loop fusion | bytes 8192 | tf_op jit(solution)/shard_map/squeeze | solution.py:288
  43.6 0.0 collective-permute-done.2.refs_2_
  43.6 0.0 collective-permute-done.3.refs_3_
  43.6 0.9 %collective-permute-done.4.refs_4_ = bf16[520,128]{1,0:T(8,128)(2,1)S(1)} collective-permute-done((bf16[520,128]{1,0:T(8,128)(2,1)S(1)}, bf16[520,128]{1,0:T(8,128)(2,1)S(1)}, u32[]{:S(2)}, u32[]{:S(2)}) %collective-permute-start.4) | collective-permute-done | bytes 133152 | tf_op jit(solution)/shard_map/ppermute | solution.py:316
  44.5 1.4 %collective-permute-done.5.refs_5_ = bf16[520,128]{1,0:T(8,128)(2,1)S(1)} collective-permute-done((bf16[520,128]{1,0:T(8,128)(2,1)S(1)}, bf16[520,128]{1,0:T(8,128)(2,1)S(1)}, u32[]{:S(2)}, u32[]{:S(2)}) %collective-permute-start.5) | collective-permute-done | bytes 133152 | tf_op jit(solution)/shard_map/ppermute | solution.py:316
  45.8 1.2 %collective-permute-done.6.refs_6_ = bf16[520,128]{1,0:T(8,128)(2,1)S(1)} collective-permute-done((bf16[520,128]{1,0:T(8,128)(2,1)S(1)}, bf16[520,128]{1,0:T(8,128)(2,1)S(1)}, u32[]{:S(2)}, u32[]{:S(2)}) %collective-permute-start.6) | collective-permute-done | bytes 133152 | tf_op jit(solution)/shard_map/ppermute | solution.py:316
  47.0 1.6 %shard_map.72 = (bf16[8,128,512]{2,1,0:T(8,128)(2,1)}, s32[8,128]{1,0:T(8,128)}, f32[2,2]{1,0:T(2,128)}) custom-call(s32[8,128]{1,0:T(8,128)S(1)} %slice_bitcast_fusion.asked_ref, f32[1,512]{1,0:T(1,128)S(1)} %get-tuple-element.19.gain_ref, s32[8,128]{1,0:T(8,128)S(1)} %get-tuple-element.22.tally_ref, bf16[512,128]{1,0:T(8,128)(2,1)S(1)} %collective-permute-done.refs_0_, ...), custom_call_target="tpu_custom_call" | custom-call | tf_op jit(solution)/shard_map/pallas_call | solution.py:227
Async XLA Ops:
  2.0 7.4 %copy-start.2 = (f32[512]{0:T(512)S(1)}, f32[512]{0:T(512)}, u32[]{:S(2)}) copy-start(f32[512]{0:T(512)} %param.7) | copy-start | bytes 6148
  2.0 14.4 %all-to-all-start = ((s32[32,1,128]{2,1,0:T(1,128)}), s32[32,1,128]{2,1,0:T(1,128)S(1)}, u32[]{:S(2)}, u32[]{:S(2)}) async-start(s32[32,1,128]{2,1,0:T(1,128)} %bitcast.12), calls=%async_computation | async-start | bytes 32768 | tf_op jit(solution)/shard_map/all_to_all | solution.py:293
  9.3 1.2 %copy-start = (bf16[1024,512]{1,0:T(8,128)(2,1)S(1)}, bf16[1024,512]{1,0:T(8,128)(2,1)}, u32[]{:S(2)}) copy-start(bf16[1024,512]{1,0:T(8,128)(2,1)} %table_ref.5) | copy-start | bytes 3145732
  10.6 5.8 %copy-start.1 = (bf16[1024,512]{1,0:T(8,128)(2,1)S(1)}, bf16[1024,512]{1,0:T(8,128)(2,1)}, u32[]{:S(2)}) copy-start(bf16[1024,512]{1,0:T(8,128)(2,1)} %table_ref.5) | copy-start | bytes 3145732
  19.4 20.8 %collective-permute-start.1 = (bf16[520,128]{1,0:T(8,128)(2,1)S(1)}, bf16[520,128]{1,0:T(8,128)(2,1)S(1)}, u32[]{:S(2)}, u32[]{:S(2)}) collective-permute-start(bf16[520,128]{1,0:T(8,128)(2,1)S(1)} %get-tuple-element.25), channel_id=1, source_target_pairs={{0,12},{4,16},{8,20},{12,24},{16,28},{20,0},{24,4},{28,8},{1,13},{... | collective-permute-start | bytes 399368 | tf_op jit(solution)/shard_map/ppermute | solution.py:316
  20.1 18.0 %collective-permute-start = (bf16[512,128]{1,0:T(8,128)(2,1)S(1)}, bf16[512,128]{1,0:T(8,128)(2,1)S(1)}, u32[]{:S(2)}, u32[]{:S(2)}) collective-permute-start(bf16[512,128]{1,0:T(8,128)(2,1)S(1)} %get-tuple-element.23), channel_id=1, source_target_pairs={{0,16},{4,20},{8,24},{12,28},{16,0},{20,4},{24,8},{28,12},{1,17},{... | collective-permute-start | bytes 393224 | tf_op jit(solution)/shard_map/ppermute | solution.py:316
  20.7 17.4 %collective-permute-start.7 = (bf16[8,128]{1,0:T(8,128)(2,1)S(1)}, bf16[8,128]{1,0:T(8,128)(2,1)S(1)}, u32[]{:S(2)}, u32[]{:S(2)}) collective-permute-start(bf16[8,128]{1,0:T(8,128)(2,1)S(1)} %get-tuple-element.24.terms_ref), channel_id=1, source_target_pairs={{0,16},{4,20},{8,24},{12,28},{16,0},{20,4},{24,8},{28,12},{1,17},{... | collective-permute-start | bytes 6152 | tf_op jit(solution)/shard_map/ppermute | solution.py:316
  23.0 20.5 %collective-permute-start.2 = (bf16[520,128]{1,0:T(8,128)(2,1)S(1)}, bf16[520,128]{1,0:T(8,128)(2,1)S(1)}, u32[]{:S(2)}, u32[]{:S(2)}) collective-permute-start(bf16[520,128]{1,0:T(8,128)(2,1)S(1)} %get-tuple-element.26), channel_id=1, source_target_pairs={{0,20},{4,24},{8,28},{12,0},{16,4},{20,8},{24,12},{28,16},{1,21},{... | collective-permute-start | bytes 399368 | tf_op jit(solution)/shard_map/ppermute | solution.py:316
  26.2 17.3 %collective-permute-start.3 = (bf16[520,128]{1,0:T(8,128)(2,1)S(1)}, bf16[520,128]{1,0:T(8,128)(2,1)S(1)}, u32[]{:S(2)}, u32[]{:S(2)}) collective-permute-start(bf16[520,128]{1,0:T(8,128)(2,1)S(1)} %get-tuple-element.27), channel_id=1, source_target_pairs={{0,8},{4,12},{8,16},{12,20},{16,24},{20,28},{24,0},{28,4},{1,9},{5... | collective-permute-start | bytes 399368 | tf_op jit(solution)/shard_map/ppermute | solution.py:316
  38.1 6.3 %collective-permute-start.4 = (bf16[520,128]{1,0:T(8,128)(2,1)S(1)}, bf16[520,128]{1,0:T(8,128)(2,1)S(1)}, u32[]{:S(2)}, u32[]{:S(2)}) collective-permute-start(bf16[520,128]{1,0:T(8,128)(2,1)S(1)} %get-tuple-element.28), channel_id=1, source_target_pairs={{0,24},{4,28},{8,0},{12,4},{16,8},{20,12},{24,16},{28,20},{1,25},{... | collective-permute-start | bytes 399368 | tf_op jit(solution)/shard_map/ppermute | solution.py:316
  38.1 7.7 %collective-permute-start.5 = (bf16[520,128]{1,0:T(8,128)(2,1)S(1)}, bf16[520,128]{1,0:T(8,128)(2,1)S(1)}, u32[]{:S(2)}, u32[]{:S(2)}) collective-permute-start(bf16[520,128]{1,0:T(8,128)(2,1)S(1)} %get-tuple-element.29), channel_id=1, source_target_pairs={{0,4},{4,8},{8,12},{12,16},{16,20},{20,24},{24,28},{28,0},{1,5},{5... | collective-permute-start | bytes 399368 | tf_op jit(solution)/shard_map/ppermute | solution.py:316
  40.2 6.8 %collective-permute-start.6 = (bf16[520,128]{1,0:T(8,128)(2,1)S(1)}, bf16[520,128]{1,0:T(8,128)(2,1)S(1)}, u32[]{:S(2)}, u32[]{:S(2)}) collective-permute-start(bf16[520,128]{1,0:T(8,128)(2,1)S(1)} %get-tuple-element.30), channel_id=1, source_target_pairs={{0,28},{4,0},{8,4},{12,8},{16,12},{20,16},{24,20},{28,24},{1,29},{... | collective-permute-start | bytes 399368 | tf_op jit(solution)/shard_map/ppermute | solution.py:316

commit v2 on v1

--- a/solution.py
+++ b/solution.py
@@ -15,6 +15,7 @@
 GRANT = 16 << 20
 WIDE_GRANT = 60 << 20
 MOST_PERMUTES = 16
+AHEAD = 1
 
 epsilon = 1e-06
 
@@ -60,7 +61,7 @@
     moments_ref[...] = jnp.transpose(columns)[: 2 * LAYERS * blocks]
 
 
-def ask_kernel(held_rows, used_hbm, requests_hbm, everywhere_hbm, used_ref, requests_ref, asked_ref, sems):
+def ask_kernel(held_rows, used_hbm, requests_hbm, asked_hbm, everywhere_hbm, used_ref, requests_ref, asked_ref, sems):
     owners, slot_count = requests_ref.shape
     copies = [
         pltpu.make_async_copy(used_hbm, used_ref, sems.at[0]),
@@ -77,8 +78,8 @@
     copies[1].wait()
     asked_ref[...] = jnp.where(slot < used, requests_ref[...], held_rows)
     copies = []
-    for group in range(everywhere_hbm.shape[0]):
-        copies.append(pltpu.make_async_copy(asked_ref, everywhere_hbm.at[group], sems.at[2 + group]))
+    for place, target in enumerate([asked_hbm] + [everywhere_hbm.at[group] for group in range(everywhere_hbm.shape[0])]):
+        copies.append(pltpu.make_async_copy(asked_ref, target, sems.at[2 + place]))
         copies[-1].start()
     for copy in copies:
         copy.wait()
@@ -134,11 +135,10 @@
     return jnp.transpose(jnp.concatenate(rows + filler, axis=0))
 
 
-def first_kernel(owners, shifts, wanted_ref, table_ref, passed_ref, *message_refs):
-    passed_ref[...] = wanted_ref[...]
-    columns = asked_of_me(owners, wanted_ref, shifts)
-    for place, message_ref in enumerate(message_refs):
-        put(message_ref, pick(table_ref, columns[:, place : place + 1]))
+def first_kernel(asked_ref, table_ref, message_ref):
+    row = asked_ref[pl.ds(lax.axis_index("rows"), 1), :]
+    column = jnp.transpose(jnp.concatenate([row] * SUBLANES, axis=0))[:, :1]
+    put(message_ref, pick(table_ref, column))
 
 
 def tally_kernel(wanted_ref, moments_ref, counts_ref, terms_ref, high_ref, low_ref):
@@ -272,27 +272,30 @@
     counts = jax.ShapeDtypeStruct((blocks, LANES), jnp.int32)
     by_permutes = slot_count == LANES and owners <= MOST_PERMUTES // 2
     if by_permutes:
-        everywhere = kernel_call(
+        asked, everywhere = kernel_call(
             functools.partial(ask_kernel, held_rows),
-            jax.ShapeDtypeStruct((groups, owners, slot_count), jnp.int32),
+            (
+                jax.ShapeDtypeStruct((owners, slot_count), jnp.int32),
+                jax.ShapeDtypeStruct((groups, owners, slot_count), jnp.int32),
+            ),
             [HBM] * 2,
-            HBM,
+            (HBM,) * 2,
             (
                 pltpu.SMEM((1, owners), jnp.int32),
                 pltpu.VMEM((owners, slot_count), jnp.int32),
                 pltpu.VMEM((owners, slot_count), jnp.int32),
-                pltpu.SemaphoreType.DMA((2 + groups,)),
+                pltpu.SemaphoreType.DMA((3 + groups,)),
             ),
             WIDE_GRANT,
         )(request_counts, requests[0])
-        asked = everywhere[0]
     else:
         slot = lax.broadcasted_iota(jnp.int32, (owners, slot_count), 1)
         asked = jnp.where(slot < request_counts[0][:, None], requests[0], held_rows)
         everywhere = jnp.broadcast_to(asked[None], (groups, owners, slot_count))
     wanted = lax.all_to_all(
         everywhere.reshape(groups * owners, slot_count), ("rep", "rows"), split_axis=0, concat_axis=0, tiled=True
-    ).reshape(-1, LANES)
+    )
+    wanted = wanted.reshape(-1, LANES)
     moments, gain = kernel_call(
         row_moments_kernel,
         (
@@ -308,32 +311,29 @@
     )
     if by_permutes:
         shifts = shifts_of(owners)
-        early = 1
 
         def send(a, shift):
             if not shift:
                 return a
             return lax.ppermute(a, "rows", [(i, (i + shift) % owners) for i in range(owners)])
 
-        wanted, *first = kernel_call(
-            functools.partial(first_kernel, owners, shifts[:early]),
-            (jax.ShapeDtypeStruct(wanted.shape, jnp.int32),) + (bare,) * early,
-            [VMEM] * 2,
-            (VMEM,) * (1 + early),
-        )(wanted, table)
-        sources = [send(a, shift) for a, shift in zip(first, shifts)]
+        sources = []
+        for shift in shifts[:AHEAD]:
+            asked_first = send(asked, -shift)
+            message_first = kernel_call(first_kernel, bare, [VMEM] * 2, VMEM)(asked_first, table)
+            sources.append(send(message_first, shift))
         tallied, terms = kernel_call(
             tally_kernel, (counts, figures), [VMEM] * 2, (VMEM,) * 2, tally_scratch
         )(wanted, moments)
         rest = kernel_call(
-            functools.partial(serve_kernel, owners, shifts[early:]),
-            (message,) * (owners - early),
+            functools.partial(serve_kernel, owners, shifts[AHEAD:]),
+            (message,) * (owners - AHEAD),
             [VMEM] * 3,
-            (VMEM,) * (owners - early),
+            (VMEM,) * (owners - AHEAD),
         )(wanted, terms, table)
-        sources += [send(a, shift) for a, shift in zip(rest, shifts[early:])]
-        sources += [send(terms, shift) for shift in shifts[:early]]
-        order = functools.partial(by_shift, shifts, early)
+        sources += [send(a, shift) for a, shift in zip(rest, shifts[AHEAD:])]
+        sources += [send(terms, shift) for shift in shifts[:AHEAD]]
+        order = functools.partial(by_shift, shifts, AHEAD)
     else:
         mine = lax.dynamic_index_in_dim(
             wanted.reshape(groups, -1, LANES), lax.axis_index("rep"), 0, False

time: 48.8 us -> 49.1 us (level)
  starting transfers between devices: 19.4 us -> 22.2 us
  waiting for transfers between devices: 19.3 us -> 17.4 us
  local copies, waits for them, and re-layouts: 1.92 us -> 1.24 us
    ppermute x8 -> x9, starting transfers between devices: 12.1 us -> 14.9 us  [send(): lax.ppermute(a, 'rows', [(i, (i + shift) % owners) for i in range(owners)])]
    all_to_all x1, waiting for transfers between devices: 4.46 us -> 1.71 us  [per_device(): lax.all_to_all(everywhere.reshape(groups * owners, slot_count), ('rep', '...]
    ppermute x8 -> x9, waiting for transfers between devices: 14.8 us -> 15.7 us  [send(): lax.ppermute(a, 'rows', [(i, (i + shift) % owners) for i in range(owners)])]
    squeeze x1 -> x0, local copies, waits for them, and re-layouts: 0.69 us -> none  [per_device(): asked = everywhere[0]]
    unnamed x6 -> x8, local copies, waits for them, and re-layouts: 1.23 us -> 1.24 us
  transfers between devices with their start and end apart: 9 -> 10, of which waited for: 5 -> 5; matrix products, arithmetic and copies ran while one was open for 1% -> 0% of each run, Pallas kernels for 3% -> 9%
where the time goes in v2:
time: 49.1 us; the launch traced here: 48.9 us
  starting transfers between devices  22.2 us (45%)
  waiting for transfers between devices  17.4 us (35%)
  Pallas kernels  7.31 us (15%)
  local copies, waits for them, and re-layouts  1.24 us (3%)
  between operations  0.71 us (1%)
    ppermute x9, waiting for transfers between devices, send(): lax.ppermute(a, 'rows', [(i, (i + shift) % owners) for i in range(owners)])  15.7 us
    ppermute x9, starting transfers between devices, send(): lax.ppermute(a, 'rows', [(i, (i + shift) % owners) for i in range(owners)])  14.9 us
    all_to_all x1, starting transfers between devices, per_device(): lax.all_to_all(everywhere.reshape(groups * owners, slot_count), ('rep', '...  7.33 us
    all_to_all x1, waiting for transfers between devices, per_device(): lax.all_to_all(everywhere.reshape(groups * owners, slot_count), ('rep', '...  1.71 us
    pallas_call x1, Pallas kernels, normalize(): kernel_call(functools.partial(normalize_kernel, order, held_rows), (jax.S...  1.55 us
    pallas_call x1, Pallas kernels, per_device(): kernel_call(row_moments_kernel, (jax.ShapeDtypeStruct((2 * LAYERS * block...  1.37 us
    pallas_call x1, Pallas kernels, per_device(): kernel_call(functools.partial(ask_kernel, held_rows), (jax.ShapeDtypeStru...  1.36 us
    pallas_call x1, Pallas kernels, per_device(): kernel_call(tally_kernel, (counts, figures), [VMEM] * 2, (VMEM,) * 2, tal...  1.31 us
  transfers between devices with their start and end apart: 10, of which 5 were waited for; matrix products, arithmetic and copies ran while one was open for 0% of the time, Pallas kernels for 9%

profile of v2, /device:TPU:0, one launch (start us, length us, event | category | flops | bytes accessed | tf_op | source)
XLA Modules:
  0.0 48.9 jit_solution(9616988163041348180)
XLA Ops:
  0.6 1.4 %shard_map.67 = (s32[8,128]{1,0:T(8,128)}, s32[4,8,128]{2,1,0:T(8,128)}) custom-call(s32[1,8]{1,0:T(1,128)} %used_hbm.1, s32[8,128]{1,0:T(8,128)} %bitcast.12), custom_call_target="tpu_custom_call" | custom-call | tf_op jit(solution)/shard_map/pallas_call | solution.py:275
  2.0 0.0 copy-start.2
  2.0 7.3 %all-to-all-start = ((s32[32,1,128]{2,1,0:T(1,128)}), s32[32,1,128]{2,1,0:T(1,128)S(1)}, u32[]{:S(2)}, u32[]{:S(2)}) async-start(s32[32,1,128]{2,1,0:T(1,128)} %bitcast.11), calls=%async_computation | async-start | bytes 32768 | tf_op jit(solution)/shard_map/all_to_all | solution.py:295
  9.3 0.0 copy-start.3
  9.4 0.0 copy-done.2
  9.4 2.7 %collective-permute-start = (s32[8,128]{1,0:T(8,128)S(1)}, s32[8,128]{1,0:T(8,128)S(1)}, u32[]{:S(2)}, u32[]{:S(2)}) collective-permute-start(s32[8,128]{1,0:T(8,128)S(1)} %copy-done.2), channel_id=1, source_target_pairs={{0,16},{4,20},{8,24},{12,28},{16,0},{20,4},{24,8},{28,12},{1,17},{... | collective-permute-start | bytes 12296 | tf_op jit(solution)/shard_map/ppermute | solution.py:318
  12.1 0.0 copy-done.3
  12.1 0.0 copy-start
  12.1 1.2 %copy-done = bf16[1024,512]{1,0:T(8,128)(2,1)S(1)} copy-done((bf16[1024,512]{1,0:T(8,128)(2,1)S(1)}, bf16[1024,512]{1,0:T(8,128)(2,1)}, u32[]{:S(2)}) %copy-start) | copy-done | bytes 1048600
  13.3 0.0 copy-start.1
  13.3 1.4 %shard_map.68 = (f32[32,128]{1,0:T(8,128)S(1)}, f32[1,512]{1,0:T(1,128)S(1)}) custom-call(bf16[1024,512]{1,0:T(8,128)(2,1)S(1)} %copy-done, f32[1,512]{1,0:T(1,128)S(1)} %bitcast.10), custom_call_target="tpu_custom_call" | custom-call | tf_op jit(solution)/shard_map/pallas_call | solution.py:299
  14.7 1.7 %all-to-all-done = s32[32,1,128]{2,1,0:T(1,128)S(1)} async-done(((s32[32,1,128]{2,1,0:T(1,128)}), s32[32,1,128]{2,1,0:T(1,128)S(1)}, u32[]{:S(2)}, u32[]{:S(2)}) %all-to-all-start) | async-done | bytes 16416 | tf_op jit(solution)/shard_map/all_to_all | solution.py:295
  16.4 1.3 %shard_map.69 = (s32[8,128]{1,0:T(8,128)S(1)}, bf16[8,128]{1,0:T(8,128)(2,1)S(1)}) custom-call(s32[32,128]{1,0:T(8,128)S(1)} %bitcast.8, f32[32,128]{1,0:T(8,128)S(1)} %get-tuple-element.22.moments_ref), custom_call_target="tpu_custom_call" | custom-call | tf_op jit(solution)/shard_map/pallas_call | solution.py:325
  17.7 0.0 copy-done.1
  17.7 1.3 %shard_map.71 = (bf16[520,128]{1,0:T(8,128)(2,1)S(1)}, bf16[520,128]{1,0:T(8,128)(2,1)S(1)}, bf16[520,128]{1,0:T(8,128)(2,1)S(1)}, bf16[520,128]{1,0:T(8,128)(2,...) custom-call(s32[32,128]{1,0:T(8,128)S(1)} %bitcast.9, ...), custom_call_target="tpu_custom_call" | custom-call | tf_op jit(solution)/shard_map/pallas_call | solution.py:328
  19.0 0.8 %collective-permute-start.2 = (bf16[520,128]{1,0:T(8,128)(2,1)S(1)}, bf16[520,128]{1,0:T(8,128)(2,1)S(1)}, u32[]{:S(2)}, u32[]{:S(2)}) collective-permute-start(bf16[520,128]{1,0:T(8,128)(2,1)S(1)} %get-tuple-element.25), channel_id=1, source_target_pairs={{0,12},{4,16},{8,20},{12,24},{16,28},{20,0},{24,4},{28,8},{1,13},{... | collective-permute-start | bytes 399368 | tf_op jit(solution)/shard_map/ppermute | solution.py:318
  19.8 0.0 collective-permute-done.asked_ref
  19.8 0.4 shard_map.70
  20.3 0.7 %collective-permute-start.1 = (bf16[512,128]{1,0:T(8,128)(2,1)S(1)}, bf16[512,128]{1,0:T(8,128)(2,1)S(1)}, u32[]{:S(2)}, u32[]{:S(2)}) collective-permute-start(bf16[512,128]{1,0:T(8,128)(2,1)S(1)} %shard_map.70), channel_id=1, source_target_pairs={{0,16},{4,20},{8,24},{12,28},{16,0},{20,4},{24,8},{28,12},{1,17},{... | collective-permute-start | bytes 393224 | tf_op jit(solution)/shard_map/ppermute | solution.py:318
  20.9 2.3 %collective-permute-start.8 = (bf16[8,128]{1,0:T(8,128)(2,1)S(1)}, bf16[8,128]{1,0:T(8,128)(2,1)S(1)}, u32[]{:S(2)}, u32[]{:S(2)}) collective-permute-start(bf16[8,128]{1,0:T(8,128)(2,1)S(1)} %get-tuple-element.24.terms_ref), channel_id=1, source_target_pairs={{0,16},{4,20},{8,24},{12,28},{16,0},{20,4},{24,8},{28,12},{1,17},{... | collective-permute-start | bytes 6152 | tf_op jit(solution)/shard_map/ppermute | solution.py:318
  23.3 3.1 %collective-permute-start.3 = (bf16[520,128]{1,0:T(8,128)(2,1)S(1)}, bf16[520,128]{1,0:T(8,128)(2,1)S(1)}, u32[]{:S(2)}, u32[]{:S(2)}) collective-permute-start(bf16[520,128]{1,0:T(8,128)(2,1)S(1)} %get-tuple-element.26), channel_id=1, source_target_pairs={{0,20},{4,24},{8,28},{12,0},{16,4},{20,8},{24,12},{28,16},{1,21},{... | collective-permute-start | bytes 399368 | tf_op jit(solution)/shard_map/ppermute | solution.py:318
  26.4 0.5 %collective-permute-start.4 = (bf16[520,128]{1,0:T(8,128)(2,1)S(1)}, bf16[520,128]{1,0:T(8,128)(2,1)S(1)}, u32[]{:S(2)}, u32[]{:S(2)}) collective-permute-start(bf16[520,128]{1,0:T(8,128)(2,1)S(1)} %get-tuple-element.27), channel_id=1, source_target_pairs={{0,8},{4,12},{8,16},{12,20},{16,24},{20,28},{24,0},{28,4},{1,9},{5... | collective-permute-start | bytes 399368 | tf_op jit(solution)/shard_map/ppermute | solution.py:318
  26.9 10.8 %collective-permute-done.8.refs_8_ = bf16[8,128]{1,0:T(8,128)(2,1)S(1)} collective-permute-done((bf16[8,128]{1,0:T(8,128)(2,1)S(1)}, bf16[8,128]{1,0:T(8,128)(2,1)S(1)}, u32[]{:S(2)}, u32[]{:S(2)}) %collective-permute-start.8) | collective-permute-done | bytes 2080 | tf_op jit(solution)/shard_map/ppermute | solution.py:318
  37.7 0.0 collective-permute-start.5
  37.7 0.0 collective-permute-done.1.refs_0_
  37.7 2.1 %collective-permute-start.6 = (bf16[520,128]{1,0:T(8,128)(2,1)S(1)}, bf16[520,128]{1,0:T(8,128)(2,1)S(1)}, u32[]{:S(2)}, u32[]{:S(2)}) collective-permute-start(bf16[520,128]{1,0:T(8,128)(2,1)S(1)} %get-tuple-element.29), channel_id=1, source_target_pairs={{0,4},{4,8},{8,12},{12,16},{16,20},{20,24},{24,28},{28,0},{1,5},{5... | collective-permute-start | bytes 399368 | tf_op jit(solution)/shard_map/ppermute | solution.py:318
  39.8 0.0 collective-permute-done.2.refs_1_
  39.8 2.6 %collective-permute-start.7 = (bf16[520,128]{1,0:T(8,128)(2,1)S(1)}, bf16[520,128]{1,0:T(8,128)(2,1)S(1)}, u32[]{:S(2)}, u32[]{:S(2)}) collective-permute-start(bf16[520,128]{1,0:T(8,128)(2,1)S(1)} %get-tuple-element.30), channel_id=1, source_target_pairs={{0,28},{4,0},{8,4},{12,8},{16,12},{20,16},{24,20},{28,24},{1,29},{... | collective-permute-start | bytes 399368 | tf_op jit(solution)/shard_map/ppermute | solution.py:318
  42.5 0.0 collective-permute-done.3.refs_2_
  42.5 0.0 collective-permute-done.4.refs_3_
  42.5 1.6 %collective-permute-done.5.refs_4_ = bf16[520,128]{1,0:T(8,128)(2,1)S(1)} collective-permute-done((bf16[520,128]{1,0:T(8,128)(2,1)S(1)}, bf16[520,128]{1,0:T(8,128)(2,1)S(1)}, u32[]{:S(2)}, u32[]{:S(2)}) %collective-permute-start.5) | collective-permute-done | bytes 133152 | tf_op jit(solution)/shard_map/ppermute | solution.py:318
  44.1 1.9 %collective-permute-done.6.refs_5_ = bf16[520,128]{1,0:T(8,128)(2,1)S(1)} collective-permute-done((bf16[520,128]{1,0:T(8,128)(2,1)S(1)}, bf16[520,128]{1,0:T(8,128)(2,1)S(1)}, u32[]{:S(2)}, u32[]{:S(2)}) %collective-permute-start.6) | collective-permute-done | bytes 133152 | tf_op jit(solution)/shard_map/ppermute | solution.py:318
  46.0 1.3 %collective-permute-done.7.refs_6_ = bf16[520,128]{1,0:T(8,128)(2,1)S(1)} collective-permute-done((bf16[520,128]{1,0:T(8,128)(2,1)S(1)}, bf16[520,128]{1,0:T(8,128)(2,1)S(1)}, u32[]{:S(2)}, u32[]{:S(2)}) %collective-permute-start.7) | collective-permute-done | bytes 133152 | tf_op jit(solution)/shard_map/ppermute | solution.py:318
  47.3 1.6 %shard_map.72 = (bf16[8,128,512]{2,1,0:T(8,128)(2,1)}, s32[8,128]{1,0:T(8,128)}, f32[2,2]{1,0:T(2,128)}) custom-call(s32[8,128]{1,0:T(8,128)S(1)} %copy-done.2, f32[1,512]{1,0:T(1,128)S(1)} %get-tuple-element.20.gain_ref, s32[8,128]{1,0:T(8,128)S(1)} %get-tuple-element.23.tally_ref, bf16[512,128]{1,0:T(8,128)(2,1)S(1)} %collective-permute-done.1.refs_0_, ...), custom_call_target="tpu_custom_call" | custom-call | tf_op jit(solution)/shard_map/pallas_call | solution.py:227
Async XLA Ops:
  2.0 7.4 %copy-start.2 = (s32[8,128]{1,0:T(8,128)S(1)}, s32[8,128]{1,0:T(8,128)}, u32[]{:S(2)}) copy-start(s32[8,128]{1,0:T(8,128)} %get-tuple-element.19.asked_ref) | copy-start | bytes 12292
  2.0 14.4 %all-to-all-start = ((s32[32,1,128]{2,1,0:T(1,128)}), s32[32,1,128]{2,1,0:T(1,128)S(1)}, u32[]{:S(2)}, u32[]{:S(2)}) async-start(s32[32,1,128]{2,1,0:T(1,128)} %bitcast.11), calls=%async_computation | async-start | bytes 32768 | tf_op jit(solution)/shard_map/all_to_all | solution.py:295
  9.3 2.8 %copy-start.3 = (f32[512]{0:T(512)S(1)}, f32[512]{0:T(512)}, u32[]{:S(2)}) copy-start(f32[512]{0:T(512)} %param.7) | copy-start | bytes 6148
  9.4 10.5 %collective-permute-start = (s32[8,128]{1,0:T(8,128)S(1)}, s32[8,128]{1,0:T(8,128)S(1)}, u32[]{:S(2)}, u32[]{:S(2)}) collective-permute-start(s32[8,128]{1,0:T(8,128)S(1)} %copy-done.2), channel_id=1, source_target_pairs={{0,16},{4,20},{8,24},{12,28},{16,0},{20,4},{24,8},{28,12},{1,17},{... | collective-permute-start | bytes 12296 | tf_op jit(solution)/shard_map/ppermute | solution.py:318
  12.1 1.2 %copy-start = (bf16[1024,512]{1,0:T(8,128)(2,1)S(1)}, bf16[1024,512]{1,0:T(8,128)(2,1)}, u32[]{:S(2)}) copy-start(bf16[1024,512]{1,0:T(8,128)(2,1)} %table_ref.5) | copy-start | bytes 3145732
  13.3 4.4 %copy-start.1 = (bf16[1024,512]{1,0:T(8,128)(2,1)S(1)}, bf16[1024,512]{1,0:T(8,128)(2,1)}, u32[]{:S(2)}) copy-start(bf16[1024,512]{1,0:T(8,128)(2,1)} %table_ref.5) | copy-start | bytes 3145732
  19.0 20.8 %collective-permute-start.2 = (bf16[520,128]{1,0:T(8,128)(2,1)S(1)}, bf16[520,128]{1,0:T(8,128)(2,1)S(1)}, u32[]{:S(2)}, u32[]{:S(2)}) collective-permute-start(bf16[520,128]{1,0:T(8,128)(2,1)S(1)} %get-tuple-element.25), channel_id=1, source_target_pairs={{0,12},{4,16},{8,20},{12,24},{16,28},{20,0},{24,4},{28,8},{1,13},{... | collective-permute-start | bytes 399368 | tf_op jit(solution)/shard_map/ppermute | solution.py:318
  20.3 17.5 %collective-permute-start.1 = (bf16[512,128]{1,0:T(8,128)(2,1)S(1)}, bf16[512,128]{1,0:T(8,128)(2,1)S(1)}, u32[]{:S(2)}, u32[]{:S(2)}) collective-permute-start(bf16[512,128]{1,0:T(8,128)(2,1)S(1)} %shard_map.70), channel_id=1, source_target_pairs={{0,16},{4,20},{8,24},{12,28},{16,0},{20,4},{24,8},{28,12},{1,17},{... | collective-permute-start | bytes 393224 | tf_op jit(solution)/shard_map/ppermute | solution.py:318
  20.9 16.8 %collective-permute-start.8 = (bf16[8,128]{1,0:T(8,128)(2,1)S(1)}, bf16[8,128]{1,0:T(8,128)(2,1)S(1)}, u32[]{:S(2)}, u32[]{:S(2)}) collective-permute-start(bf16[8,128]{1,0:T(8,128)(2,1)S(1)} %get-tuple-element.24.terms_ref), channel_id=1, source_target_pairs={{0,16},{4,20},{8,24},{12,28},{16,0},{20,4},{24,8},{28,12},{1,17},{... | collective-permute-start | bytes 6152 | tf_op jit(solution)/shard_map/ppermute | solution.py:318
  23.3 19.2 %collective-permute-start.3 = (bf16[520,128]{1,0:T(8,128)(2,1)S(1)}, bf16[520,128]{1,0:T(8,128)(2,1)S(1)}, u32[]{:S(2)}, u32[]{:S(2)}) collective-permute-start(bf16[520,128]{1,0:T(8,128)(2,1)S(1)} %get-tuple-element.26), channel_id=1, source_target_pairs={{0,20},{4,24},{8,28},{12,0},{16,4},{20,8},{24,12},{28,16},{1,21},{... | collective-permute-start | bytes 399368 | tf_op jit(solution)/shard_map/ppermute | solution.py:318
  26.4 16.1 %collective-permute-start.4 = (bf16[520,128]{1,0:T(8,128)(2,1)S(1)}, bf16[520,128]{1,0:T(8,128)(2,1)S(1)}, u32[]{:S(2)}, u32[]{:S(2)}) collective-permute-start(bf16[520,128]{1,0:T(8,128)(2,1)S(1)} %get-tuple-element.27), channel_id=1, source_target_pairs={{0,8},{4,12},{8,16},{12,20},{16,24},{20,28},{24,0},{28,4},{1,9},{5... | collective-permute-start | bytes 399368 | tf_op jit(solution)/shard_map/ppermute | solution.py:318
  37.7 6.3 %collective-permute-start.5 = (bf16[520,128]{1,0:T(8,128)(2,1)S(1)}, bf16[520,128]{1,0:T(8,128)(2,1)S(1)}, u32[]{:S(2)}, u32[]{:S(2)}) collective-permute-start(bf16[520,128]{1,0:T(8,128)(2,1)S(1)} %get-tuple-element.28), channel_id=1, source_target_pairs={{0,24},{4,28},{8,0},{12,4},{16,8},{20,12},{24,16},{28,20},{1,25},{... | collective-permute-start | bytes 399368 | tf_op jit(solution)/shard_map/ppermute | solution.py:318
  37.7 8.3 %collective-permute-start.6 = (bf16[520,128]{1,0:T(8,128)(2,1)S(1)}, bf16[520,128]{1,0:T(8,128)(2,1)S(1)}, u32[]{:S(2)}, u32[]{:S(2)}) collective-permute-start(bf16[520,128]{1,0:T(8,128)(2,1)S(1)} %get-tuple-element.29), channel_id=1, source_target_pairs={{0,4},{4,8},{8,12},{12,16},{16,20},{20,24},{24,28},{28,0},{1,5},{5... | collective-permute-start | bytes 399368 | tf_op jit(solution)/shard_map/ppermute | solution.py:318
  39.8 7.5 %collective-permute-start.7 = (bf16[520,128]{1,0:T(8,128)(2,1)S(1)}, bf16[520,128]{1,0:T(8,128)(2,1)S(1)}, u32[]{:S(2)}, u32[]{:S(2)}) collective-permute-start(bf16[520,128]{1,0:T(8,128)(2,1)S(1)} %get-tuple-element.30), channel_id=1, source_target_pairs={{0,28},{4,0},{8,4},{12,8},{16,12},{20,16},{24,20},{28,24},{1,29},{... | collective-permute-start | bytes 399368 | tf_op jit(solution)/shard_map/ppermute | solution.py:318
